TPU v7x, 256 devices: a whole 4x4x8 slice. The times are simulated.
256 devices in a mesh: seq: 128 (over y, x_lo, z, core), dp: 2 (over x_hi).
Axes of the slice: x: 4 (x_hi: 2, x_lo: 2; x = x_hi * 2 + x_lo), y: 4, z: 8, core: 2. Of those that a mesh axis runs over, the one named last changes fastest.
Arguments:
- q_student: bfloat16 [2, 65536, 1536], P('dp', 'seq'), may hold values from -8 to 8
- kv_student: bfloat16 [2, 1024, 3072], P('dp', 'seq'), may hold values from -8 to 8
- q_target: bfloat16 [2, 65536, 1536], P('dp', 'seq'), may hold values from -8 to 8
- kv_target: bfloat16 [2, 1024, 3072], P('dp', 'seq'), may hold values from -8 to 8
Outputs:
- student_out: bfloat16 [2, 65536, 1536], P('dp', 'seq')
- target_out: bfloat16 [2, 65536, 1536], P('dp', 'seq')
- distill_loss: float32 [], replicated
All inputs are finite; a program needn't handle non-finite values.
Results may differ from a plain program's by a relative error of at most 0.004.
Values may be sent and summed in bfloat16 or wider, within the bound.
A program may use at most 128 MiB of HBM per device.

v0:
```python
import functools
import heapq

import jax
import jax.numpy as jnp
from jax import lax
from jax.experimental import pallas as pl
from jax.experimental.pallas import tpu as pltpu
from jax.sharding import PartitionSpec as P

HEADS = 12
HD = 128
WIDTH = HEADS * HD
NY, NX, NZ = 4, 2, 8
SIZE = {"y": NY, "x": NX, "z": NZ}
AXIS = {"y": 0, "x": 1, "z": 2}
ROWS = 8
SLOTS = 2 * NY * NX * NZ
LINES = NY * NX
LOG2E = 1.4426950408889634
UNITS = 2 * HEADS
GROUPS = (
    ("yxz", 0, 4, 9.0, 2, 0),
    ("zxy", 0, 4, 1.0, 1, 1),
    ("yxz", 0, 3, 0.0, 1, 2),
    ("zxy", 1, 3, 0.0, 0, 2),
    ("zxy", 0, 5, 12.0, 1, 1),
    ("yzx", 1, 5, 1.0, 2, 0),
)
LATENCY = 3.0
FIRST = [sum(g[2] for g in GROUPS[:i]) for i in range(len(GROUPS))]
KEEP = 3


def signed(axis, v, d, salt):
    n = SIZE[axis]
    if axis == "x":
        return v
    if v * 2 == n:
        return v if (sum(d) - v + salt) % 2 == 0 else -v
    return v if v * 2 < n else v - n


def children(order, d, salt, jump):
    out = []
    for axis in "zyx":
        for s in (2, -2, 1, -1) if axis != "x" else (1,):
            nd = list(d)
            nd[AXIS[axis]] = (nd[AXIS[axis]] + s) % SIZE[axis]
            nd = tuple(nd)
            if nd == (0, 0, 0) or axis != next(a for a in reversed(order) if nd[AXIS[a]]):
                continue
            v = signed(axis, nd[AXIS[axis]], nd, salt)
            step = 2 if v % 2 == 0 and order.index(axis) < jump else 1
            if s == (step if v > 0 else -step):
                out.append((axis, s, nd))
    return out


def height(order, d, salt, jump):
    return max([1 + height(order, c[2], salt, jump) for c in children(order, d, salt, jump)] or [0])


def plan():
    pend, ready, free, log, count, now, held = [], [], {}, [], 0, 0.0, False
    got, done, left = [0] * len(GROUPS), [None] * len(GROUPS), [g[2] for g in GROUPS]
    for k, g in enumerate(GROUPS):
        heapq.heappush(pend, (g[3], count, k, (0, 0, 0)))
        count += 1
    while pend or ready or any(left) or held:
        while pend and pend[0][0] <= now:
            at, _, k, d = heapq.heappop(pend)
            name, salt, _, _, rank, jump = GROUPS[k]
            heapq.heappush(ready, ((rank, -height(name, d, salt, jump), at), k, d))
        if ready:
            _, k, d = heapq.heappop(ready)
            name, salt, units, _, _, jump = GROUPS[k]
            kids = sorted(children(name, d, salt, jump), key=lambda c: -height(name, c[2], salt, jump))
            log.append(("relay", k, d, kids))
            now += 0.016
            for axis, s, nd in kids:
                now += 0.016
                way = (axis, s > 0)
                busy = units * 4096 / 46.7e3
                start = max(now, free.get(way, 0.0))
                free[way] = start + abs(s) * busy
                heapq.heappush(pend, (start + busy + LATENCY + 0.8 * (abs(s) - 1), count, k, nd))
                count += 1
            got[k] += 1
            if got[k] == NY * NX * NZ:
                done[k] = now + 1.6
            continue
        open_groups = [k for k in range(len(GROUPS)) if left[k] and done[k] is not None]
        best = min(open_groups, key=lambda k: done[k], default=None)
        if best is not None and done[best] <= now:
            log.append(("unit", best, GROUPS[best][2] - left[best]))
            left[best] -= 1
            now += 0.7 if held else 0.4
            held = True
            continue
        later = min([p[0] for p in pend[:1]] + [done[k] for k in open_groups], default=now + 9)
        if held and later > now + 0.3:
            log.append(("flush",))
            now += 0.55
            held = False
            continue
        now = later
    return log


def score(q, buf, unit, kk, scores):
    keys = SLOTS * ROWS
    kk[...] = buf[:, 2 * unit].astype(jnp.float32).reshape(keys, HD).astype(jnp.bfloat16)
    for at in range(0, keys, 256):
        scores[:, at : at + 256] = lax.dot_general(
            q, kk[at : at + 256], (((1,), (1,)), ((), ())), preferred_element_type=jnp.float32
        )


def mix(buf, unit, vv, scores, block):
    vv[:, :HD] = buf[:, 2 * unit + 1].astype(jnp.float32).reshape(SLOTS * ROWS, HD).astype(jnp.bfloat16)
    outs = []
    for r in range(0, scores.shape[0], block):
        part = scores[r : r + block]
        part = (part - jnp.max(part, axis=1, keepdims=True)) * (LOG2E / HD**0.5)
        expo = jnp.exp2(part).astype(jnp.bfloat16)
        mixed = jnp.dot(expo, vv[...], preferred_element_type=jnp.float32)
        outs.append(mixed[:, :HD] / mixed[:, HD:])
    return outs


def kernel(
    qs_hbm, kvs_hbm, qt_hbm, kvt_hbm, outs, outt, loss_ref,
    buf, qs, qt, kk, vv, scores, other, acc,
    total_in, total_out, load_sem, q_sem, ici_send, d2d_send, ici_recv, d2d_recv, sum_send, sum_recv,
):
    seq = lax.axis_index("seq")
    dp = lax.axis_index("dp")
    core = lax.rem(seq, 2)
    z = lax.rem(seq // 2, NZ)
    x = lax.rem(seq // (2 * NZ), NX)
    y = seq // (2 * NZ * NX)

    def device(yy, xx, zz, cc, dd=dp):
        return {"seq": ((yy * NX + xx) * NZ + zz) * 2 + cc, "dp": dd}

    def line(cc, yy, xx):
        return ((cc * NY + yy) * NX + xx) * NZ

    near = {
        ("z", 1): device(y, x, lax.rem(z + 1, NZ), core),
        ("z", -1): device(y, x, lax.rem(z + NZ - 1, NZ), core),
        ("z", 2): device(y, x, lax.rem(z + 2, NZ), core),
        ("z", -2): device(y, x, lax.rem(z + NZ - 2, NZ), core),
        ("y", 1): device(lax.rem(y + 1, NY), x, z, core),
        ("y", -1): device(lax.rem(y + NY - 1, NY), x, z, core),
        ("y", 2): device(lax.rem(y + 2, NY), x, z, core),
        ("y", -2): device(lax.rem(y + 2, NY), x, z, core),
        ("x", 1): device(y, 1 - x, z, core),
    }
    partner = device(y, x, z, 1 - core)
    ys = [lax.rem(y + NY - d, NY) for d in range(NY)]
    xs = [x, 1 - x]
    zs = [lax.rem(z + NZ - d, NZ) for d in range(NZ)]

    cube = []
    for i in range(1, 8):
        cube.append(device(y, lax.rem(x + i // 4, 2), z, lax.rem(core + i // 2 % 2, 2), lax.rem(dp + i % 2, 2)))
    plane = [
        device(lax.rem(y + i // NZ, NY), x, lax.rem(z + i % NZ, NZ), core) for i in range(1, NY * NZ)
    ]
    sums = ((y * NZ + z, plane), ((x * 2 + core) * 2 + dp, cube))
    peers = [to for way, to in near.items() if way not in (("y", -2), ("x", 1))] + cube

    mine = line(core, y, x) + z
    barrier = pltpu.get_barrier_semaphore()
    for peer in peers:
        pl.semaphore_signal(barrier, inc=1, device_id=peer, device_id_type=pl.DeviceIdType.MESH)
    for unit in range(UNITS):
        head, kv = unit // 2, (kvs_hbm, kvt_hbm)[unit % 2]
        for part in range(2):
            cols = pl.ds(part * WIDTH + head * HD, HD)
            pltpu.make_async_copy(kv.at[0, :, cols], buf.at[mine, 2 * unit + part], load_sem.at[0]).start()
    load_q = [
        pltpu.make_async_copy(qs_hbm.at[0], qs, q_sem.at[0]),
        pltpu.make_async_copy(qt_hbm.at[0], qt, q_sem.at[1]),
    ]
    for c in load_q:
        c.start()
    vv[:, :, HD:] = jnp.ones((KEEP, SLOTS * ROWS, HD), jnp.bfloat16)
    acc[...] = jnp.zeros_like(acc)
    pltpu.make_async_copy(buf.at[mine], buf.at[mine], load_sem.at[0]).wait()
    pl.semaphore_wait(barrier, len(peers))

    def remote(part, send, recv, to):
        return pltpu.make_async_remote_copy(
            src_ref=part, dst_ref=part, send_sem=send, recv_sem=recv,
            device_id=to, device_id_type=pl.DeviceIdType.MESH,
        )

    def cut(k):
        return pl.ds(2 * FIRST[k], 2 * GROUPS[k][2])

    def item(k, d):
        return buf.at[line(core, ys[d[0]], xs[d[1]]) + zs[d[2]], cut(k)]

    def sem_of(k, d):
        return ici_recv.at[k, (d[0] * NX + d[1]) * NZ + d[2]]

    rows = qs.shape[0]
    block = 256
    have, ran, seen, loaded = {}, 0, set(), False

    def finish(unit, slot):
        head, model = unit // 2, unit % 2
        cols = slice(head * HD, head * HD + HD)
        for i, r in enumerate(mix(buf, unit, vv.at[slot], scores.at[slot], block)):
            at = slice(i * block, i * block + block)
            (outs, outt)[model][0, at, cols] = r.astype(jnp.bfloat16)
            if head in seen:
                gap = other[head, at, :] - r
                acc[at, :] += gap * gap
            else:
                other[head, at, :] = r
        seen.add(head)

    held = None
    for kind, *what in plan():
        if kind == "flush":
            finish(*held)
            held = None
            continue
        if kind == "unit":
            k, d = what
            if not loaded:
                for c in load_q:
                    c.wait()
                loaded = True
            if d == 0:
                part = buf.at[pl.ds((1 - core) * LINES * NZ, LINES * NZ), cut(k)]
                remote(part, d2d_send.at[k], d2d_recv.at[k], partner).wait_recv()
            unit = FIRST[k] + d
            slot = ran % KEEP
            ran += 1
            score((qs, qt)[unit % 2][:, unit // 2 * HD : unit // 2 * HD + HD], buf, unit, kk.at[slot], scores.at[slot])
            if held:
                finish(*held)
            held = (unit, slot)
            continue
        k, d, kids = what
        if d != (0, 0, 0):
            remote(item(k, d), ici_send.at[k], sem_of(k, d), partner).wait_recv()
        for axis, s, nd in kids:
            remote(item(k, d), ici_send.at[k], sem_of(k, nd), near[(axis, s)]).start()
        spot = (k, d[0], d[1])
        have[spot] = have.get(spot, 0) + 1
        if have[spot] == NZ:
            part = buf.at[pl.ds(line(core, ys[d[0]], xs[d[1]]), NZ), cut(k)]
            remote(part, d2d_send.at[k], d2d_recv.at[k], partner).start()

    spot = lax.broadcasted_iota(jnp.int32, (rows, HD), 0) + ((y * NX + x) * NZ + z) * 2 * rows + core * rows
    weight = 1.0 + 2.0 * spot.astype(jnp.float32) / float(rows * SLOTS - 1)
    total = jnp.sum((weight * acc[...]).reshape(rows // 8, 8, HD), axis=0)
    for i, (spot, group) in enumerate(sums):
        total_out[i] = total
        total_in[i, spot] = total
        for to in group:
            pltpu.make_async_remote_copy(
                src_ref=total_out.at[i], dst_ref=total_in.at[i, spot], send_sem=sum_send.at[i],
                recv_sem=sum_recv.at[i], device_id=to, device_id_type=pl.DeviceIdType.MESH,
            ).start()
        every = total_in.at[i, pl.ds(0, len(group))]
        remote(every, sum_send.at[i], sum_recv.at[i], partner).wait()
        total = jnp.sum(total_in[i, : len(group) + 1], axis=0)
    loss_ref[...] = total

    for k in range(len(GROUPS)):
        part = buf.at[pl.ds(0, LINES * NZ - 1), cut(k)]
        remote(part, ici_send.at[k], d2d_recv.at[k], partner).wait_send()
        part = buf.at[pl.ds(0, LINES * NZ), cut(k)]
        remote(part, d2d_send.at[k], d2d_recv.at[k], partner).wait_send()


def write(count, s_ref, t_ref, total_ref, os_hbm, ot_hbm, loss_ref, sem):
    copies = [
        pltpu.make_async_copy(s_ref, os_hbm, sem.at[0]),
        pltpu.make_async_copy(t_ref, ot_hbm, sem.at[1]),
    ]
    for c in copies:
        c.start()
    loss_ref[0] = jnp.sum(total_ref[...]) / count
    for c in copies:
        c.wait()


def body(q_student, kv_student, q_target, kv_target):
    rows = q_student.shape[1]
    bf = jnp.bfloat16
    any_space = pl.BlockSpec(memory_space=pl.ANY)
    vmem = pl.BlockSpec(memory_space=pltpu.VMEM)
    student, target, total = pl.pallas_call(
        kernel,
        out_shape=(
            pltpu.VMEM(q_student.shape, bf),
            pltpu.VMEM(q_student.shape, bf),
            pltpu.VMEM((8, HD), jnp.float32),
        ),
        in_specs=[any_space] * 4,
        out_specs=(vmem,) * 3,
        scratch_shapes=[
            pltpu.VMEM((SLOTS, 2 * UNITS, ROWS, HD), bf),
            pltpu.VMEM((rows, WIDTH), bf),
            pltpu.VMEM((rows, WIDTH), bf),
            pltpu.VMEM((KEEP, SLOTS * ROWS, HD), bf),
            pltpu.VMEM((KEEP, SLOTS * ROWS, 2 * HD), bf),
            pltpu.VMEM((KEEP, rows, SLOTS * ROWS), jnp.float32),
            pltpu.VMEM((HEADS, rows, HD), jnp.float32),
            pltpu.VMEM((rows, HD), jnp.float32),
            pltpu.VMEM((2, NY * NZ, 8, HD), jnp.float32),
            pltpu.VMEM((2, 8, HD), jnp.float32),
            pltpu.SemaphoreType.DMA((1,)),
            pltpu.SemaphoreType.DMA((2,)),
            pltpu.SemaphoreType.DMA((len(GROUPS),)),
            pltpu.SemaphoreType.DMA((len(GROUPS),)),
            pltpu.SemaphoreType.DMA((len(GROUPS), LINES * NZ)),
            pltpu.SemaphoreType.DMA((len(GROUPS),)),
            pltpu.SemaphoreType.DMA((2,)),
            pltpu.SemaphoreType.DMA((2,)),
        ],
        compiler_params=pltpu.CompilerParams(
            collective_id=0, has_side_effects=True, vmem_limit_bytes=52 * 1024 * 1024
        ),
    )(q_student, kv_student, q_target, kv_target)
    student, target, loss = pl.pallas_call(
        functools.partial(write, float(rows * SLOTS * WIDTH)),
        out_shape=(
            jax.ShapeDtypeStruct(q_student.shape, bf),
            jax.ShapeDtypeStruct(q_student.shape, bf),
            jax.ShapeDtypeStruct((1,), jnp.float32),
        ),
        in_specs=[vmem] * 3,
        out_specs=(any_space, any_space, pl.BlockSpec(memory_space=pltpu.SMEM)),
        scratch_shapes=[pltpu.SemaphoreType.DMA((2,))],
        compiler_params=pltpu.CompilerParams(vmem_limit_bytes=16 * 1024 * 1024),
    )(student, target, total)
    return student, target, loss.reshape(())


def solution(mesh):
    spec = P("dp", "seq", None)
    return jax.shard_map(
        body, mesh=mesh, in_specs=(spec,) * 4, out_specs=(spec, spec, P()), check_vma=False
    )
```

profile of v0, /device:TPU:1, one launch (start us, length us, event | category | flops | bytes accessed | tf_op | source)
XLA Modules:
  0.0 71.9 jit_solution(8875260389360415011)
XLA Ops:
  0.6 68.9 %shard_map.67 = (bf16[1,512,1536]{2,1,0:T(8,128)(2,1)S(1)}, bf16[1,512,1536]{2,1,0:T(8,128)(2,1)S(1)}, f32[8,128]{1,0:T(8,128)S(1)}) custom-call(bf16[1,512,1536]{2,1,0:T(8,128)(2,1)} %qs_hbm.1, bf16[1,8,3072]{2,1,0:T(8,128)(2,1)} %kvs_hbm.1, bf16[1,512,1536]{2,1,0:T(8,128)(2,1)} %qt_hbm.1, bf16[1,8,3072]{2,1,0:T(8,128)(2,1)} %kvt_hbm.1), custom_call_target="tpu_custom_call" | custom-call | tf_op jit(solution)/shard_map/pallas_call | solution.py:301
  69.6 2.2 %shard_map.68 = (bf16[1,512,1536]{2,1,0:T(8,128)(2,1)}, bf16[1,512,1536]{2,1,0:T(8,128)(2,1)}, f32[1]{0:T(128)}) custom-call(bf16[1,512,1536]{2,1,0:T(8,128)(2,1)S(1)} %get-tuple-element.9.s_ref, bf16[1,512,1536]{2,1,0:T(8,128)(2,1)S(1)} %get-tuple-element.10.t_ref, f32[8,128]{1,0:T(8,128)S(1)} %get-tuple-element.11.total_ref), custom_call_target="tpu_custom_call" | custom-call | tf_op jit(solution)/shard_map/pallas_call | solution.py:334
where the time goes:
time: 72 us; the launch traced here: 71.9 us
  Pallas kernels  71.1 us (99%)
  between operations  0.8 us (1%)
    pallas_call x1, Pallas kernels, body(): pl.pallas_call(kernel, out_shape=(pltpu.VMEM(q_student.shape, bf), pltpu....  68.9 us
    pallas_call x1, Pallas kernels, body(): pl.pallas_call(functools.partial(write, float(rows * SLOTS * WIDTH)), out...  2.2 us

commit v1 on v0

--- a/solution.py
+++ b/solution.py
@@ -260,7 +260,7 @@
 
     spot = lax.broadcasted_iota(jnp.int32, (rows, HD), 0) + ((y * NX + x) * NZ + z) * 2 * rows + core * rows
     weight = 1.0 + 2.0 * spot.astype(jnp.float32) / float(rows * SLOTS - 1)
-    total = jnp.sum((weight * acc[...]).reshape(rows // 8, 8, HD), axis=0)
+    total = jnp.sum(weight * acc[...], axis=0, keepdims=True)
     for i, (spot, group) in enumerate(sums):
         total_out[i] = total
         total_in[i, spot] = total
@@ -303,7 +303,7 @@
         out_shape=(
             pltpu.VMEM(q_student.shape, bf),
             pltpu.VMEM(q_student.shape, bf),
-            pltpu.VMEM((8, HD), jnp.float32),
+            pltpu.VMEM((1, HD), jnp.float32),
         ),
         in_specs=[any_space] * 4,
         out_specs=(vmem,) * 3,
@@ -316,8 +316,8 @@
             pltpu.VMEM((KEEP, rows, SLOTS * ROWS), jnp.float32),
             pltpu.VMEM((HEADS, rows, HD), jnp.float32),
             pltpu.VMEM((rows, HD), jnp.float32),
-            pltpu.VMEM((2, NY * NZ, 8, HD), jnp.float32),
-            pltpu.VMEM((2, 8, HD), jnp.float32),
+            pltpu.VMEM((2, NY * NZ, 1, HD), jnp.float32),
+            pltpu.VMEM((2, 1, HD), jnp.float32),
             pltpu.SemaphoreType.DMA((1,)),
             pltpu.SemaphoreType.DMA((2,)),
             pltpu.SemaphoreType.DMA((len(GROUPS),)),

time: 72 us -> 71 us (0.986)
  Pallas kernels: 71.1 us -> 70.2 us
    pallas_call x1, Pallas kernels: 68.9 us -> 68 us  [body(): pl.pallas_call(kernel, out_shape=(pltpu.VMEM(q_student.shape, bf), pltpu....]
where the time goes in v1:
time: 71 us
  Pallas kernels  70.2 us (99%)
  between operations  0.8 us (1%)
    pallas_call x1, Pallas kernels, body(): pl.pallas_call(kernel, out_shape=(pltpu.VMEM(q_student.shape, bf), pltpu....  68 us
    pallas_call x1, Pallas kernels, body(): pl.pallas_call(functools.partial(write, float(rows * SLOTS * WIDTH)), out...  2.2 us

profile of v1, /device:TPU:1, one launch (start us, length us, event | category | flops | bytes accessed | tf_op | source)
XLA Modules:
  0.0 71.0 jit_solution(14037700454409130885)
XLA Ops:
  0.6 68.0 %shard_map.67 = (bf16[1,512,1536]{2,1,0:T(8,128)(2,1)S(1)}, bf16[1,512,1536]{2,1,0:T(8,128)(2,1)S(1)}, f32[1,128]{1,0:T(1,128)S(1)}) custom-call(bf16[1,512,1536]{2,1,0:T(8,128)(2,1)} %qs_hbm.1, bf16[1,8,3072]{2,1,0:T(8,128)(2,1)} %kvs_hbm.1, bf16[1,512,1536]{2,1,0:T(8,128)(2,1)} %qt_hbm.1, bf16[1,8,3072]{2,1,0:T(8,128)(2,1)} %kvt_hbm.1), custom_call_target="tpu_custom_call" | custom-call | tf_op jit(solution)/shard_map/pallas_call | solution.py:301
  68.6 2.2 %shard_map.68 = (bf16[1,512,1536]{2,1,0:T(8,128)(2,1)}, bf16[1,512,1536]{2,1,0:T(8,128)(2,1)}, f32[1]{0:T(128)}) custom-call(bf16[1,512,1536]{2,1,0:T(8,128)(2,1)S(1)} %get-tuple-element.9.s_ref, bf16[1,512,1536]{2,1,0:T(8,128)(2,1)S(1)} %get-tuple-element.10.t_ref, f32[1,128]{1,0:T(1,128)S(1)} %get-tuple-element.11.total_ref), custom_call_target="tpu_custom_call" | custom-call | tf_op jit(solution)/shard_map/pallas_call | solution.py:334
